TPU v7x, 32 devices: a whole 2x2x4 slice. The times are simulated.
32 devices in a mesh: cuts: 8 (over z, y), batch: 4 (over x, core).
Axes of the slice: x: 2, y: 2, z: 4, core: 2. Of those that a mesh axis runs over, the one named last changes fastest.
Arguments:
- blocks: bfloat16 [256, 64, 128], P(('cuts', 'batch')), may hold values from -6 to 6
- environments: bfloat16 [256, 64, 128], P(('cuts', 'batch')), may hold values from -0.5 to 0.5
- layers: bfloat16 [8, 64, 128], replicated, may hold values from -0.5 to 0.5
- selectors: bfloat16 [256, 8, 128], P(('cuts', 'batch')), may hold values from -6 to 6
- classes: int32 [32, 8], P(('cuts', 'batch')), may hold values from 1 to 8
- routing: int32 [32, 8], P(('cuts', 'batch')), may hold values from 0 to 7, each once within a row
- left_edges: bfloat16 [64, 128], replicated, may hold values from -0.5 to 0.5
- right_edges: bfloat16 [64, 128], replicated, may hold values from -0.5 to 0.5
- owner_map: int32 [4096], replicated, may hold values from 0 to 4095, each once
Outputs:
- amplitudes: float32 [2, 4096], P(None, ('cuts', 'batch'))
Inputs may be any that keep to these rules, and one draw needn't show every extreme that they name: `routing`: each holder's row is a permutation of 0 to 7. `owner_map`: A permutation of the bitstrings.
All inputs are finite; a program needn't handle non-finite values.
Results may differ from a plain program's by a relative error of at most 0.009.
Values may be sent and summed in bfloat16 or wider, within the bound.
A program may use at most 64 MiB of HBM per device.

v0:
```python
import jax
import jax.numpy as jnp
from jax import lax
from jax.sharding import PartitionSpec as P


def block_form(matrix):
    half_count = matrix.shape[-1] // 2
    real_block = matrix[..., :half_count]
    imag_block = matrix[..., half_count:]
    upper_rows = jnp.concatenate([real_block, imag_block], axis=-1)
    lower_rows = jnp.concatenate([-imag_block, real_block], axis=-1)
    return jnp.concatenate([upper_rows, lower_rows], axis=-2)


def apply_phase(product, factors):
    half_count = product.shape[-1] // 2
    prod_real = product[..., :half_count]
    prod_imag = product[..., half_count:]
    fac_real = factors[..., :half_count].astype(jnp.float32)[:, None, :]
    fac_imag = factors[..., half_count:].astype(jnp.float32)[:, None, :]
    out_real = prod_real * fac_real - prod_imag * fac_imag
    out_imag = prod_real * fac_imag + prod_imag * fac_real
    return jnp.concatenate([out_real, out_imag], axis=-1)


def advance(blocks_now, factors, levels, tables):
    slot_count = blocks_now.shape[0]
    block_rows = min(32, slot_count)
    ranking = jnp.argsort(-levels, stable=True)
    blocks_now = blocks_now[ranking]
    factors = factors[ranking]
    levels = levels[ranking]
    for layer_index in range(tables.shape[0]):
        active = jnp.sum((levels > layer_index).astype(jnp.int32))
        rounds = (active + block_rows - 1) // block_rows
        layer_factors = factors[:, layer_index, :]

        def apply(round_index, current, layer_index=layer_index, layer_factors=layer_factors):
            offset = round_index * block_rows
            portion = lax.dynamic_slice_in_dim(current, offset, block_rows, 0)
            portion_levels = lax.dynamic_slice_in_dim(levels, offset, block_rows, 0)
            portion_factors = lax.dynamic_slice_in_dim(layer_factors, offset, block_rows, 0)
            product = jnp.einsum(
                "sij,jk->sik", portion, tables[layer_index], preferred_element_type=jnp.float32
            )
            updated = apply_phase(product, portion_factors).astype(jnp.bfloat16)
            portion = jnp.where((portion_levels > layer_index)[:, None, None], updated, portion)
            return lax.dynamic_update_slice_in_dim(current, portion, offset, 0)

        blocks_now = lax.fori_loop(0, rounds, apply, blocks_now)
    return (blocks_now, ranking)


def contract(worked, partners):
    slot_count, bond_width, doubled = worked.shape
    parted = worked.reshape(slot_count, bond_width, 2, bond_width)
    products = jnp.einsum("sipj,sjk->pik", parted, partners, preferred_element_type=jnp.float32)
    real_part = products[0, :, :bond_width] - products[1, :, bond_width:]
    imag_part = products[0, :, bond_width:] + products[1, :, :bond_width]
    return (real_part, imag_part)


def amplitude_table(real_part, imag_part, left_edges, right_edges, owner_map):
    highest = lax.Precision.HIGHEST
    half_count = left_edges.shape[1] // 2
    left_real = left_edges[:, :half_count].astype(jnp.float32)
    left_imag = left_edges[:, half_count:].astype(jnp.float32)
    right_real = right_edges[:, :half_count].astype(jnp.float32)
    right_imag = right_edges[:, half_count:].astype(jnp.float32)
    wave_real = jnp.dot(real_part, right_real, precision=highest) - jnp.dot(
        imag_part, right_imag, precision=highest
    )
    wave_imag = jnp.dot(real_part, right_imag, precision=highest) + jnp.dot(
        imag_part, right_real, precision=highest
    )
    amp_real = jnp.dot(left_real.T, wave_real, precision=highest) - jnp.dot(
        left_imag.T, wave_imag, precision=highest
    )
    amp_imag = jnp.dot(left_real.T, wave_imag, precision=highest) + jnp.dot(
        left_imag.T, wave_real, precision=highest
    )
    flattened = jnp.stack([amp_real.reshape(-1), amp_imag.reshape(-1)])
    return flattened[:, owner_map]


def on_device(
    blocks, environments, layers, selectors, classes, routing, left_edges, right_edges, owner_map
):
    slot_count, bond_width, doubled = blocks.shape
    cut_count = lax.axis_size("cuts")
    member = slot_count // cut_count
    tables = block_form(layers)
    levels = classes[0]
    sending = routing[0]
    worked, ranking = advance(blocks, selectors, levels, tables)
    inverse = jnp.argsort(ranking)
    outgoing = worked[inverse[sending]].reshape(cut_count, member, bond_width, doubled)
    worked = lax.all_to_all(outgoing, "cuts", split_axis=0, concat_axis=0, tiled=True).reshape(
        slot_count, bond_width, doubled
    )
    real_part, imag_part = contract(worked, environments)
    holder_count = cut_count * lax.axis_size("batch")
    normalizer = (slot_count * holder_count) ** (-0.5)
    real_part, imag_part = lax.psum((real_part, imag_part), ("cuts", "batch"))
    amp_table = (
        amplitude_table(real_part, imag_part, left_edges, right_edges, owner_map) * normalizer
    )
    per_holder = amp_table.shape[1] // holder_count
    holder = lax.axis_index("cuts") * lax.axis_size("batch") + lax.axis_index("batch")
    return lax.dynamic_slice_in_dim(amp_table, holder * per_holder, per_holder, 1)


def solution(mesh):
    placed = (
        P(("cuts", "batch"), None, None),
        P(("cuts", "batch"), None, None),
        P(),
        P(("cuts", "batch"), None, None),
        P(("cuts", "batch"), None),
        P(("cuts", "batch"), None),
        P(),
        P(),
        P(),
    )
    return jax.shard_map(
        on_device, mesh=mesh, in_specs=placed, out_specs=P(None, ("cuts", "batch")), check_vma=False
    )
```

profile of v0, /device:TPU:0, one launch (start us, length us, event | category | flops | bytes accessed | tf_op | source)
XLA Modules:
  0.0 92.2 jit_solution(10878997560112806243)
XLA Ops:
  0.0 0.7 bitcast_negate_fusion
  0.7 1.0 %sort.34 = (s32[8]{0:T(128)}, s32[8]{0:T(128)S(1)}) sort(s32[8]{0:T(128)S(1)} %bitcast_negate_fusion, s32[8]{0:T(128)S(1)} %iota.8), dimensions={0}, to_apply=%region_0.0 | sort | flops 24 | bytes 128 | tf_op jit(solution)/shard_map/jit(argsort)/sort | solution.py:30
  1.7 1.3 %gather_fusion.1 = s32[8]{0:T(128)S(1)} fusion(s32[8]{0:T(128)} %bitcast.127, s32[1024]{0:T(1024)S(1)} %pad_clamp_fusion.2), kind=kCustom, calls=%fused_computation.1 | custom fusion | bytes 96 | tf_op jit(solution)/shard_map/gather | solution.py:33
  3.0 0.8 fusion.51
  8.8 1.3 %gather_fusion.2 = bf16[8,8,128]{2,1,0:T(8,128)(2,1)S(1)} fusion(bf16[8,8,128]{2,1,0:T(8,128)(2,1)} %param.28, s32[1024]{0:T(1024)S(1)} %pad_clamp_fusion.2), kind=kCustom, calls=%fused_computation.2 | custom fusion | bytes 32800 | tf_op jit(solution)/shard_map/gather | solution.py:32
  10.1 1.1 %slice_negate_fusion = (bf16[8,64,64]{2,1,0:T(8,128)(2,1)S(1)}, bf16[8,64,64]{2,1,0:T(8,128)(2,1)S(1)}) fusion(bf16[8,64,128]{2,1,0:T(8,128)(2,1)} %param.27), kind=kLoop, calls=%fused_computation.88 | loop fusion | flops 32768 | bytes 262144 | tf_op jit(solution)/shard_map/neg | solution.py:12
  11.2 0.6 gather_fusion
  11.8 1.0 %maximum_maximum_fusion = bf16[8,128,128]{2,1,0:T(8,128)(2,1)S(1)} fusion(bf16[8,64,64]{2,1,0:T(8,128)(2,1)S(1)} %get-tuple-element.420, bf16[8,64,64]{2,1,0:T(8,128)(2,1)S(1)} %get-tuple-element.419, bf16[8,64,128]{2,1,0:T(8,128)(2,1)} %param.27), kind=kLoop, calls=%fused_computation.85 | loop fusion | flops 786432 | bytes 524288 | tf_op jit(solution)/shard_map/concatenate | solution.py:13
  12.8 0.6 while.80
  13.5 0.6 while.81
  14.1 0.6 while.82
  15.0 1.0 %sort.35 = (s32[8]{0:T(128)}, s32[8]{0:T(128)S(1)}) sort(s32[8]{0:T(128)S(1)} %get-tuple-element.271, s32[8]{0:T(128)S(1)} %iota.9), dimensions={0}, to_apply=%region_25.26 | sort | flops 24 | bytes 128 | tf_op jit(solution)/shard_map/jit(argsort)/sort | solution.py:97
  16.0 0.6 gather_fusion.3
  16.6 1.2 %gather_fusion.4 = bf16[8,64,128]{2,1,0:T(8,128)(2,1)} fusion(bf16[8,64,128]{2,1,0:T(8,128)(2,1)S(1)} %get-tuple-element.279, s32[1024]{0:T(1024)S(1)} %pad_clamp_fusion), kind=kCustom, calls=%fused_computation.4 | custom fusion | bytes 262176 | tf_op jit(solution)/shard_map/gather | solution.py:98
  17.8 10.2 %all-to-all-start = ((bf16[8,1,64,128]{3,2,1,0:T(8,128)(2,1)}), bf16[8,1,64,128]{3,2,1,0:T(8,128)(2,1)S(1)}, u32[]{:S(2)}, u32[]{:S(2)}) async-start(bf16[8,1,64,128]{3,2,1,0:T(8,128)(2,1)} %bitcast.21), calls=%async_computation | async-start | bytes 262144 | tf_op jit(solution)/shard_map/all_to_all | solution.py:99
  28.1 7.3 %all-to-all-done = bf16[8,1,64,128]{3,2,1,0:T(8,128)(2,1)S(1)} async-done(((bf16[8,1,64,128]{3,2,1,0:T(8,128)(2,1)}), bf16[8,1,64,128]{3,2,1,0:T(8,128)(2,1)S(1)}, u32[]{:S(2)}, u32[]{:S(2)}) %all-to-all-start) | async-done | bytes 131104 | tf_op jit(solution)/shard_map/all_to_all | solution.py:99
  35.5 0.2 convolution_bitcast_fusion
  35.9 38.0 %all-reduce = (f32[64,64]{1,0:T(8,128)S(1)}, f32[64,64]{1,0:T(8,128)S(1)}) all-reduce(f32[64,64]{1,0:T(8,128)S(1)} %get-tuple-element.422, f32[64,64]{1,0:T(8,128)S(1)} %get-tuple-element.421), channel_id=1, replica_groups=mesh['cuts'=8,'batch'=4] {'cuts','batch'}, use_global_device_ids=true, to_apply=%region_26.27 | all-reduce | flops 8192 | bytes 65536 | tf_op jit(solution)/shard_map/psum | solution.py:105
  75.1 0.2 fusion.25
  75.5 0.2 fusion.24
  76.0 0.6 copy.26
  76.6 14.1 %gather_fusion.5 = f32[4096,2]{1,0:T(8,128)} fusion(f32[2,4096]{0,1:T(8,128)S(1)} %copy.26, s32[4096]{0:T(1024)S(1)} %fusion.31), kind=kCustom, calls=%fused_computation.5 | custom fusion | bytes 81920 | tf_op jit(solution)/shard_map/gather | solution.py:84
  90.7 0.8 fusion.28
  91.6 0.6 copy.27
  (59 shorter events, 3.6 us)
Async XLA Ops:
  0.0 11.2 %copy-start = (bf16[8,64,128]{2,1,0:T(8,128)(2,1)S(1)}, bf16[8,64,128]{2,1,0:T(8,128)(2,1)}, u32[]{:S(2)}) copy-start(bf16[8,64,128]{2,1,0:T(8,128)(2,1)} %param.25) | copy-start | bytes 393220
  14.9 1.1 %copy-start.5 = (s32[1,8]{1,0:T(1,128)S(1)}, s32[1,8]{1,0:T(1,128)}, u32[]{:S(2)}) copy-start(s32[1,8]{1,0:T(1,128)} %param.30) | copy-start | bytes 100
  14.9 13.1 %copy-start.3 = (s32[4096]{0:T(1024)S(1)}, s32[4096]{0:T(1024)}, u32[]{:S(2)}) copy-start(s32[4096]{0:T(1024)} %param.33) | copy-start | bytes 49156
  14.9 20.6 %copy-start.4 = (bf16[8,64,128]{2,1,0:T(8,128)(2,1)S(1)}, bf16[8,64,128]{2,1,0:T(8,128)(2,1)}, u32[]{:S(2)}) copy-start(bf16[8,64,128]{2,1,0:T(8,128)(2,1)} %param.26) | copy-start | bytes 393220
  15.0 59.0 %copy-start.1 = (bf16[64,128]{1,0:T(8,128)(2,1)S(1)}, bf16[64,128]{1,0:T(8,128)(2,1)}, u32[]{:S(2)}) copy-start(bf16[64,128]{1,0:T(8,128)(2,1)} %param.32) | copy-start | bytes 49156
  15.0 59.7 %copy-start.2 = (bf16[64,128]{1,0:T(8,128)(2,1)S(1)}, bf16[64,128]{1,0:T(8,128)(2,1)}, u32[]{:S(2)}) copy-start(bf16[64,128]{1,0:T(8,128)(2,1)} %param.31) | copy-start | bytes 49156
  17.8 17.6 %all-to-all-start = ((bf16[8,1,64,128]{3,2,1,0:T(8,128)(2,1)}), bf16[8,1,64,128]{3,2,1,0:T(8,128)(2,1)S(1)}, u32[]{:S(2)}, u32[]{:S(2)}) async-start(bf16[8,1,64,128]{3,2,1,0:T(8,128)(2,1)} %bitcast.21), calls=%async_computation | async-start | bytes 262144 | tf_op jit(solution)/shard_map/all_to_all | solution.py:99
where the time goes:
time: 92.8 us; the launch traced here: 92.2 us
  blocking collectives  38 us (41%)
  local copies, waits for them, and re-layouts  20.9 us (23%)
  starting transfers between devices  10.2 us (11%)
  other arithmetic  7.64 us (8%)
  waiting for transfers between devices  7.32 us (8%)
  between operations  5.54 us (6%)
  matrix products  2.34 us (3%)
    psum x1, blocking collectives, on_device(): real_part, imag_part = lax.psum((real_part, imag_part), ('cuts', 'batch'))  38 us
    gather x1, local copies, waits for them, and re-layouts, amplitude_table(): return flattened[:, owner_map]  14.1 us
    all_to_all x1, starting transfers between devices, on_device(): lax.all_to_all(outgoing, 'cuts', split_axis=0, concat_axis=0, tiled=True)  10.2 us
    all_to_all x1, waiting for transfers between devices, on_device(): lax.all_to_all(outgoing, 'cuts', split_axis=0, concat_axis=0, tiled=True)  7.32 us
  transfers between devices with their start and end apart: 1, of which 1 were waited for; matrix products, arithmetic and copies ran while one was open for 0% of the time, Pallas kernels for 0%

commit v1 on v0

--- a/solution.py
+++ b/solution.py
@@ -2,6 +2,29 @@
 import jax.numpy as jnp
 from jax import lax
 from jax.sharding import PartitionSpec as P
+
+
+def cut_along(x, dim, size):
+    shape = x.shape
+    parts = x.reshape(*shape[:dim], size, shape[dim] // size, *shape[dim + 1 :])
+    return jnp.moveaxis(parts, dim, 0)
+
+
+def joined_along(blocks, dim):
+    blocks = jnp.moveaxis(blocks, 0, dim)
+    shape = blocks.shape
+    return blocks.reshape(*shape[:dim], shape[dim] * shape[dim + 1], *shape[dim + 2 :])
+
+
+def rotated_exchange(x, axis, split_dim, concat_dim):
+    size, index = (lax.axis_size(axis), lax.axis_index(axis))
+    blocks = cut_along(x, split_dim, size)
+    outs = [blocks[index]]
+    for turn in range(1, size):
+        sent = blocks[(index + turn) % size]
+        outs.append(lax.ppermute(sent, axis, [(i, (i + turn) % size) for i in range(size)]))
+    blocks = jnp.stack(outs)[(index - jnp.arange(size)) % size]
+    return joined_along(blocks, concat_dim)
 
 
 def block_form(matrix):
@@ -96,9 +119,7 @@
     worked, ranking = advance(blocks, selectors, levels, tables)
     inverse = jnp.argsort(ranking)
     outgoing = worked[inverse[sending]].reshape(cut_count, member, bond_width, doubled)
-    worked = lax.all_to_all(outgoing, "cuts", split_axis=0, concat_axis=0, tiled=True).reshape(
-        slot_count, bond_width, doubled
-    )
+    worked = rotated_exchange(outgoing, "cuts", 0, 0).reshape(slot_count, bond_width, doubled)
     real_part, imag_part = contract(worked, environments)
     holder_count = cut_count * lax.axis_size("batch")
     normalizer = (slot_count * holder_count) ** (-0.5)

time: 92.8 us -> 104 us (1.12)
  waiting for transfers between devices: 7.32 us -> 15.9 us
  starting transfers between devices: 10.2 us -> 13.9 us
  other arithmetic: 7.64 us -> 6.6 us
    ppermute x0 -> x7, waiting for transfers between devices: none -> 15.9 us  [rotated_exchange(): lax.ppermute(sent, axis, [(i, (i + turn) % size) for i in range(size)])]
    ppermute x0 -> x7, starting transfers between devices: none -> 13.9 us  [rotated_exchange(): lax.ppermute(sent, axis, [(i, (i + turn) % size) for i in range(size)])]
    all_to_all x1 -> x0, starting transfers between devices: 10.2 us -> none  [on_device(): lax.all_to_all(outgoing, 'cuts', split_axis=0, concat_axis=0, tiled=True)]
    all_to_all x1 -> x0, waiting for transfers between devices: 7.32 us -> none  [on_device(): lax.all_to_all(outgoing, 'cuts', split_axis=0, concat_axis=0, tiled=True)]
  transfers between devices with their start and end apart: 1 -> 7, of which waited for: 1 -> 3; matrix products, arithmetic and copies ran while one was open for 0% -> 0% of each run, Pallas kernels for 0% -> 0%
where the time goes in v1:
time: 104 us; the launch traced here: 103 us
  blocking collectives  37.3 us (36%)
  local copies, waits for them, and re-layouts  21 us (20%)
  waiting for transfers between devices  15.9 us (15%)
  starting transfers between devices  13.9 us (13%)
  other arithmetic  6.6 us (6%)
  between operations  5.71 us (5%)
  matrix products  2.34 us (2%)
    psum x1, blocking collectives, on_device(): real_part, imag_part = lax.psum((real_part, imag_part), ('cuts', 'batch'))  37.3 us
    ppermute x7, waiting for transfers between devices, rotated_exchange(): lax.ppermute(sent, axis, [(i, (i + turn) % size) for i in range(size)])  15.9 us
    gather x1, local copies, waits for them, and re-layouts, amplitude_table(): return flattened[:, owner_map]  14.1 us
    ppermute x7, starting transfers between devices, rotated_exchange(): lax.ppermute(sent, axis, [(i, (i + turn) % size) for i in range(size)])  13.9 us
  transfers between devices with their start and end apart: 7, of which 3 were waited for; matrix products, arithmetic and copies ran while one was open for 0% of the time, Pallas kernels for 0%

profile of v1, /device:TPU:0, one launch (start us, length us, event | category | flops | bytes accessed | tf_op | source)
XLA Modules:
  0.0 103.0 jit_solution(4827590776523225360)
XLA Ops:
  0.0 0.7 fusion.53
  0.7 0.7 bitcast_negate_fusion
  1.4 1.0 %sort.34 = (s32[8]{0:T(128)}, s32[8]{0:T(128)S(1)}) sort(s32[8]{0:T(128)S(1)} %bitcast_negate_fusion, s32[8]{0:T(128)S(1)} %iota.12), dimensions={0}, to_apply=%region_0.0 | sort | flops 24 | bytes 128 | tf_op jit(solution)/shard_map/jit(argsort)/sort | solution.py:53
  2.4 1.0 %sort.35 = (s32[8]{0:T(128)}, s32[8]{0:T(128)S(1)}) sort(s32[8]{0:T(128)S(1)} %get-tuple-element.271, s32[8]{0:T(128)S(1)} %iota.13), dimensions={0}, to_apply=%region_25.26 | sort | flops 24 | bytes 128 | tf_op jit(solution)/shard_map/jit(argsort)/sort | solution.py:120
  3.4 0.6 gather_fusion.3
  4.1 1.3 %gather_fusion.1 = s32[8]{0:T(128)S(1)} fusion(s32[8]{0:T(128)} %bitcast.165, s32[1024]{0:T(1024)S(1)} %get-tuple-element.439), kind=kCustom, calls=%fused_computation.1 | custom fusion | bytes 96 | tf_op jit(solution)/shard_map/gather | solution.py:56
  5.4 0.8 fusion.51
  11.4 1.3 %gather_fusion.2 = bf16[8,8,128]{2,1,0:T(8,128)(2,1)S(1)} fusion(bf16[8,8,128]{2,1,0:T(8,128)(2,1)} %param.28, s32[1024]{0:T(1024)S(1)} %get-tuple-element.439), kind=kCustom, calls=%fused_computation.2 | custom fusion | bytes 32800 | tf_op jit(solution)/shard_map/gather | solution.py:55
  12.8 0.6 gather_fusion
  13.6 0.6 while.80
  14.2 0.6 while.81
  14.8 0.6 while.82
  16.2 9.0 %collective-permute-start.6 = (bf16[1,1,64,128]{3,2,1,0:T(8,128)(2,1)S(1)}, bf16[1,1,64,128]{3,2,1,0:T(8,128)(2,1)S(1)}, u32[]{:S(2)}, u32[]{:S(2)}) collective-permute-start(bf16[1,1,64,128]{3,2,1,0:T(8,128)(2,1)S(1)} %get-tuple-element.419), channel_id=1, source_target_pairs={{0,28},{4,0},{8,4},{12,8},{16,12},{20,16},{24,20},{28,24},{1,29},{... | collective-permute-start | bytes 49160 | tf_op jit(solution)/shard_map/ppermute | solution.py:25
  25.2 3.4 %collective-permute-start.3 = (bf16[1,1,64,128]{3,2,1,0:T(8,128)(2,1)S(1)}, bf16[1,1,64,128]{3,2,1,0:T(8,128)(2,1)S(1)}, u32[]{:S(2)}, u32[]{:S(2)}) collective-permute-start(bf16[1,1,64,128]{3,2,1,0:T(8,128)(2,1)S(1)} %get-tuple-element.422), channel_id=1, source_target_pairs={{0,16},{4,20},{8,24},{12,28},{16,0},{20,4},{24,8},{28,12},{1,17},{... | collective-permute-start | bytes 49160 | tf_op jit(solution)/shard_map/ppermute | solution.py:25
  28.6 1.5 %collective-permute-start = (bf16[1,1,64,128]{3,2,1,0:T(8,128)(2,1)S(1)}, bf16[1,1,64,128]{3,2,1,0:T(8,128)(2,1)S(1)}, u32[]{:S(2)}, u32[]{:S(2)}) collective-permute-start(bf16[1,1,64,128]{3,2,1,0:T(8,128)(2,1)S(1)} %get-tuple-element.425), channel_id=1, source_target_pairs={{0,4},{4,8},{8,12},{12,16},{16,20},{20,24},{24,28},{28,0},{1,5},{5... | collective-permute-start | bytes 49160 | tf_op jit(solution)/shard_map/ppermute | solution.py:25
  30.2 4.8 %collective-permute-done = bf16[1,1,64,128]{3,2,1,0:T(8,128)(2,1)S(1)} collective-permute-done((bf16[1,1,64,128]{3,2,1,0:T(8,128)(2,1)S(1)}, bf16[1,1,64,128]{3,2,1,0:T(8,128)(2,1)S(1)}, u32[]{:S(2)}, u32[]{:S(2)}) %collective-permute-start) | collective-permute-done | bytes 16416 | tf_op jit(solution)/shard_map/ppermute | solution.py:25
  35.1 5.5 %collective-permute-done.1 = bf16[1,1,64,128]{3,2,1,0:T(8,128)(2,1)S(1)} collective-permute-done((bf16[1,1,64,128]{3,2,1,0:T(8,128)(2,1)S(1)}, bf16[1,1,64,128]{3,2,1,0:T(8,128)(2,1)S(1)}, u32[]{:S(2)}, u32[]{:S(2)}) %collective-permute-start.1) | collective-permute-done | bytes 16416 | tf_op jit(solution)/shard_map/ppermute | solution.py:25
  40.6 5.5 %collective-permute-done.2 = bf16[1,1,64,128]{3,2,1,0:T(8,128)(2,1)S(1)} collective-permute-done((bf16[1,1,64,128]{3,2,1,0:T(8,128)(2,1)S(1)}, bf16[1,1,64,128]{3,2,1,0:T(8,128)(2,1)S(1)}, u32[]{:S(2)}, u32[]{:S(2)}) %collective-permute-start.2) | collective-permute-done | bytes 16416 | tf_op jit(solution)/shard_map/ppermute | solution.py:25
  46.2 0.6 gather_fusion.5
  47.3 37.3 %all-reduce = (f32[64,64]{1,0:T(8,128)S(1)}, f32[64,64]{1,0:T(8,128)S(1)}) all-reduce(f32[64,64]{1,0:T(8,128)S(1)} %get-tuple-element.429, f32[64,64]{1,0:T(8,128)S(1)} %get-tuple-element.428), channel_id=1, replica_groups=mesh['cuts'=8,'batch'=4] {'cuts','batch'}, use_global_device_ids=true, to_apply=%region_26.27 | all-reduce | flops 8192 | bytes 65536 | tf_op jit(solution)/shard_map/psum | solution.py:126
  86.7 0.7 copy.26
  87.4 14.1 %gather_fusion.6 = f32[4096,2]{1,0:T(8,128)} fusion(f32[2,4096]{0,1:T(8,128)S(1)} %copy.26, s32[4096]{0:T(1024)S(1)} %fusion.31), kind=kCustom, calls=%fused_computation.6 | custom fusion | bytes 81920 | tf_op jit(solution)/shard_map/gather | solution.py:107
  101.5 0.8 fusion.28
  102.3 0.6 copy.27
  (86 shorter events, 5.2 us)
Async XLA Ops:
  0.0 12.8 %copy-start = (bf16[8,64,128]{2,1,0:T(8,128)(2,1)S(1)}, bf16[8,64,128]{2,1,0:T(8,128)(2,1)}, u32[]{:S(2)}) copy-start(bf16[8,64,128]{2,1,0:T(8,128)(2,1)} %param.25) | copy-start | bytes 393220
  0.0 13.4 %copy-start.1 = (bf16[8,64,128]{2,1,0:T(8,128)(2,1)S(1)}, bf16[8,64,128]{2,1,0:T(8,128)(2,1)}, u32[]{:S(2)}) copy-start(bf16[8,64,128]{2,1,0:T(8,128)(2,1)} %param.27) | copy-start | bytes 393220
  15.5 14.7 %copy-start.4 = (s32[4096]{0:T(1024)S(1)}, s32[4096]{0:T(1024)}, u32[]{:S(2)}) copy-start(s32[4096]{0:T(1024)} %param.33) | copy-start | bytes 49156
  15.5 31.4 %copy-start.5 = (bf16[8,64,128]{2,1,0:T(8,128)(2,1)S(1)}, bf16[8,64,128]{2,1,0:T(8,128)(2,1)}, u32[]{:S(2)}) copy-start(bf16[8,64,128]{2,1,0:T(8,128)(2,1)} %param.26) | copy-start | bytes 393220
  15.6 69.1 %copy-start.2 = (bf16[64,128]{1,0:T(8,128)(2,1)S(1)}, bf16[64,128]{1,0:T(8,128)(2,1)}, u32[]{:S(2)}) copy-start(bf16[64,128]{1,0:T(8,128)(2,1)} %param.32) | copy-start | bytes 49156
  15.6 69.8 %copy-start.3 = (bf16[64,128]{1,0:T(8,128)(2,1)S(1)}, bf16[64,128]{1,0:T(8,128)(2,1)}, u32[]{:S(2)}) copy-start(bf16[64,128]{1,0:T(8,128)(2,1)} %param.31) | copy-start | bytes 49156
  16.2 30.0 %collective-permute-start.6 = (bf16[1,1,64,128]{3,2,1,0:T(8,128)(2,1)S(1)}, bf16[1,1,64,128]{3,2,1,0:T(8,128)(2,1)S(1)}, u32[]{:S(2)}, u32[]{:S(2)}) collective-permute-start(bf16[1,1,64,128]{3,2,1,0:T(8,128)(2,1)S(1)} %get-tuple-element.419), channel_id=1, source_target_pairs={{0,28},{4,0},{8,4},{12,8},{16,12},{20,16},{24,20},{28,24},{1,29},{... | collective-permute-start | bytes 49160 | tf_op jit(solution)/shard_map/ppermute | solution.py:25
  25.2 21.0 %collective-permute-start.5 = (bf16[1,1,64,128]{3,2,1,0:T(8,128)(2,1)S(1)}, bf16[1,1,64,128]{3,2,1,0:T(8,128)(2,1)S(1)}, u32[]{:S(2)}, u32[]{:S(2)}) collective-permute-start(bf16[1,1,64,128]{3,2,1,0:T(8,128)(2,1)S(1)} %get-tuple-element.420), channel_id=1, source_target_pairs={{0,24},{4,28},{8,0},{12,4},{16,8},{20,12},{24,16},{28,20},{1,25},{... | collective-permute-start | bytes 49160 | tf_op jit(solution)/shard_map/ppermute | solution.py:25
  25.2 21.0 %collective-permute-start.4 = (bf16[1,1,64,128]{3,2,1,0:T(8,128)(2,1)S(1)}, bf16[1,1,64,128]{3,2,1,0:T(8,128)(2,1)S(1)}, u32[]{:S(2)}, u32[]{:S(2)}) collective-permute-start(bf16[1,1,64,128]{3,2,1,0:T(8,128)(2,1)S(1)} %get-tuple-element.421), channel_id=1, source_target_pairs={{0,20},{4,24},{8,28},{12,0},{16,4},{20,8},{24,12},{28,16},{1,21},{... | collective-permute-start | bytes 49160 | tf_op jit(solution)/shard_map/ppermute | solution.py:25
  25.2 21.0 %collective-permute-start.3 = (bf16[1,1,64,128]{3,2,1,0:T(8,128)(2,1)S(1)}, bf16[1,1,64,128]{3,2,1,0:T(8,128)(2,1)S(1)}, u32[]{:S(2)}, u32[]{:S(2)}) collective-permute-start(bf16[1,1,64,128]{3,2,1,0:T(8,128)(2,1)S(1)} %get-tuple-element.422), channel_id=1, source_target_pairs={{0,16},{4,20},{8,24},{12,28},{16,0},{20,4},{24,8},{28,12},{1,17},{... | collective-permute-start | bytes 49160 | tf_op jit(solution)/shard_map/ppermute | solution.py:25
  28.6 6.4 %collective-permute-start = (bf16[1,1,64,128]{3,2,1,0:T(8,128)(2,1)S(1)}, bf16[1,1,64,128]{3,2,1,0:T(8,128)(2,1)S(1)}, u32[]{:S(2)}, u32[]{:S(2)}) collective-permute-start(bf16[1,1,64,128]{3,2,1,0:T(8,128)(2,1)S(1)} %get-tuple-element.425), channel_id=1, source_target_pairs={{0,4},{4,8},{8,12},{12,16},{16,20},{20,24},{24,28},{28,0},{1,5},{5... | collective-permute-start | bytes 49160 | tf_op jit(solution)/shard_map/ppermute | solution.py:25
  35.1 5.5 %collective-permute-start.1 = (bf16[1,1,64,128]{3,2,1,0:T(8,128)(2,1)S(1)}, bf16[1,1,64,128]{3,2,1,0:T(8,128)(2,1)S(1)}, u32[]{:S(2)}, u32[]{:S(2)}) collective-permute-start(bf16[1,1,64,128]{3,2,1,0:T(8,128)(2,1)S(1)} %get-tuple-element.424), channel_id=1, source_target_pairs={{0,8},{4,12},{8,16},{12,20},{16,24},{20,28},{24,0},{28,4},{1,9},{5... | collective-permute-start | bytes 49160 | tf_op jit(solution)/shard_map/ppermute | solution.py:25
  40.6 5.5 %collective-permute-start.2 = (bf16[1,1,64,128]{3,2,1,0:T(8,128)(2,1)S(1)}, bf16[1,1,64,128]{3,2,1,0:T(8,128)(2,1)S(1)}, u32[]{:S(2)}, u32[]{:S(2)}) collective-permute-start(bf16[1,1,64,128]{3,2,1,0:T(8,128)(2,1)S(1)} %get-tuple-element.423), channel_id=1, source_target_pairs={{0,12},{4,16},{8,20},{12,24},{16,28},{20,0},{24,4},{28,8},{1,13},{... | collective-permute-start | bytes 49160 | tf_op jit(solution)/shard_map/ppermute | solution.py:25
